TPU v7x, 32 devices: a whole 2x2x4 slice. The times are simulated.
32 devices in a mesh: wave: 2 (over x), plane: 16 (over z, y, core).
Axes of the slice: x: 2, y: 2, z: 4, core: 2. Of those that a mesh axis runs over, the one named last changes fastest.
Arguments:
- right_side: float32 [2, 128, 128], P('wave', 'plane'), may hold values from -40 to 40
- coupling_x: float32 [128, 128], P('plane'), may hold values from 2 to 6
- coupling_y: float32 [2, 128], P('wave'), may hold values from 0.2 to 0.6
- coupling_z: float32 [2, 128, 128], P('wave', 'plane'), may hold values from 0.3 to 1
- inverse: float32 [2, 128, 128, 128], P('wave', 'plane'), may hold values from -0.05 to 0.15
Outputs:
- solution: float32 [2, 128, 128], P('wave', 'plane')
- residual: float32 [2, 128, 128], P('wave', 'plane')
All inputs are finite; a program needn't handle non-finite values.
Results may differ from a plain program's by a relative error of at most 0.0003.
Values sent between devices are 32-bit elements; how exact they have to be, the bound alone decides.
A program may use at most 64 MiB of HBM per device.

v0:
```python
import jax
import jax.numpy as jnp
from jax import lax
from jax.sharding import PartitionSpec as P

ITERS = 2


relax = 1.5


def extended(cells, sides, width):
    for axis, dim in sides:
        count = lax.axis_size(axis)
        ends = count - 1
        head = lax.slice_in_dim(cells, 0, width, axis=dim)
        tail = lax.slice_in_dim(cells, cells.shape[dim] - width, cells.shape[dim], axis=dim)
        cells = jnp.concatenate(
            [
                lax.ppermute(tail, axis, [(i, (i + 1) % count) for i in range(ends)]),
                cells,
                lax.ppermute(head, axis, [((i + 1) % count, i) for i in range(ends)]),
            ],
            axis=dim,
        )
    return cells


def passed_along(block, axis, distance):
    devices = range(lax.axis_size(axis))
    route = [(i - distance, i) for i in devices if i - distance in devices]
    return lax.ppermute(block, axis, route)


def apply_block(block, vector):
    return jnp.einsum("cij,cj->ci", block, vector, precision=lax.Precision.HIGHEST)


def column_part(values, coupling_x, coupling_y, coupling_z):
    below = jnp.concatenate([jnp.zeros_like(values[..., :1]), values[..., :-1]], axis=-1)
    above = jnp.concatenate([values[..., 1:], jnp.zeros_like(values[..., :1])], axis=-1)
    upper_z = jnp.concatenate([coupling_z[..., 1:], coupling_z[..., :1]], axis=-1)
    centre = 2.0 * coupling_x[None] + 2.0 * coupling_y[:, None] + coupling_z + upper_z
    return centre * values - coupling_z * below - upper_z * above


def operate(values, coupling_x, coupling_y, coupling_z):
    padded = extended(values, (("wave", 0), ("plane", 1)), 1)
    along_x = padded[:-2, 1:-1] + padded[2:, 1:-1]
    along_y = padded[1:-1, :-2] + padded[1:-1, 2:]
    return (
        column_part(values, coupling_x, coupling_y, coupling_z)
        - coupling_x[None] * along_x
        - coupling_y[:, None] * along_y
    )


def sweep_planes(source, inverse, coupling, incoming, base, backward):
    depth = source.shape[0]
    order = range(depth - 1, -1, -1) if backward else range(depth)
    planes = [None] * depth
    previous = incoming
    for layer_index in order:
        update = relax * apply_block(
            inverse[layer_index], source[layer_index] + coupling * previous
        )
        previous = update if base is None else base[layer_index] + update
        planes[layer_index] = previous
    return jnp.stack(planes)


def relay(source, inverse, coupling_x, base, groups, backward):
    sections = lax.axis_size("wave")
    position = lax.axis_index("wave")
    depth, columns, blocks = source.shape
    width = columns // groups
    order_index = sections - 1 - position if backward else position

    def advance(turn_index, state_tuple, send):
        incoming, result, arrived = state_tuple
        group_index = turn_index - order_index
        active = jnp.logical_and(group_index >= 0, group_index < groups)
        start = jnp.clip(group_index, 0, groups - 1) * width

        def working(operands):
            incoming_part, result_now, arrived_now = operands
            base_part = None if base is None else base
            planes = sweep_planes(source, inverse, coupling_x, incoming_part, base_part, backward)
            result_now = lax.dynamic_update_slice_in_dim(result_now, planes, start, 1)
            arrived_now = incoming_part
            outgoing_plane = planes[0] if backward else planes[depth - 1]
            return (result_now, arrived_now, outgoing_plane)

        def waiting(operands):
            return (operands[1], operands[2], jnp.zeros_like(operands[0]))

        result, arrived, outgoing = lax.cond(active, working, waiting, (incoming, result, arrived))
        if send:
            if backward:
                incoming = passed_along(outgoing, "wave", -1)
            else:
                incoming = passed_along(outgoing, "wave", 1)
        return (incoming, result, arrived)

    def looping(turn_index, state_tuple):
        return advance(turn_index, state_tuple, True)

    initial = (
        jnp.zeros((width, blocks), jnp.float32),
        jnp.zeros_like(source),
        jnp.zeros((columns, blocks), jnp.float32),
    )
    state_tuple = lax.fori_loop(0, sections + groups - 2, looping, initial)
    state_tuple = advance(sections + groups - 2, state_tuple, False)
    return (state_tuple[1], state_tuple[2])


def precondition(residual, inverse, coupling_x, coupling_y, coupling_z, groups):
    half_sweep, arrived = relay(residual, inverse, coupling_x, None, groups, False)
    lower_x = jnp.concatenate([arrived[None], half_sweep[:-1]], axis=0)
    framed = extended(half_sweep, (("plane", 1),), 1)
    settled = (
        column_part(half_sweep, coupling_x, coupling_y, coupling_z) - coupling_x[None] * lower_x
    )
    settled = settled - coupling_y[:, None] * (framed[:, :-2] + framed[:, 2:])
    result, unused = relay(residual - settled, inverse, coupling_x, half_sweep, groups, True)
    return result


def on_device(right_side, coupling_x, coupling_y, coupling_z, inverse):
    groups = 1
    solution = jnp.zeros_like(right_side)
    residual = right_side
    direction = right_side
    image = right_side
    curvature = jnp.float32(1.0)
    for iteration in range(ITERS):
        precond = precondition(residual, inverse, coupling_x, coupling_y, coupling_z, groups)
        applied = operate(precond, coupling_x, coupling_y, coupling_z)
        if iteration == 0:
            across_term = jnp.float32(0.0)
            older_term = jnp.float32(0.0)
        else:
            across_term = jnp.sum(precond * image)
            older_term = jnp.sum(direction * residual)
        across, own_part, older_part, energy = lax.psum(
            (across_term, jnp.sum(precond * residual), older_term, jnp.sum(precond * applied)),
            ("wave", "plane"),
        )
        if iteration == 0:
            direction = precond
            image = applied
            projection = own_part
            curvature = energy
        else:
            ratio = -across / curvature
            direction = precond + ratio * direction
            image = applied + ratio * image
            projection = own_part + ratio * older_part
            curvature = energy + 2.0 * ratio * across + ratio * ratio * curvature
        step_size = projection / curvature
        solution = solution + step_size * direction
        residual = residual - step_size * image
    return (solution, residual)


def solution(mesh):
    placed = (
        P("wave", "plane", None),
        P("plane", None),
        P("wave", None),
        P("wave", "plane", None),
        P("wave", "plane", None, None),
    )
    return jax.shard_map(
        on_device,
        mesh=mesh,
        in_specs=placed,
        out_specs=(P("wave", "plane", None), P("wave", "plane", None)),
        check_vma=False,
    )
```

profile of v0, /device:TPU:0, one launch (start us, length us, event | category | flops | bytes accessed | tf_op | source)
XLA Modules:
  0.0 177.7 jit_solution(4682367006670908270)
XLA Ops:
  1.3 2.0 %conditional.8 = (f32[1,8,128]{2,1,0:T(8,128)S(1)}, f32[8,128]{1,0:T(8,128)S(1)}, f32[8,128]{1,0:T(8,128)S(1)}) conditional(s32[]{:T(128)} %convert_element_type.23, (f32[1,8,128]{2,1,0:T(8,128)}, f32[8,128]{1,0:T(8,128)S(1)}) %tuple.92, (f32[1,8,128]{2,1,0:T(8,128)S(1)}, f32[8,128]{1,0:T(8,128)S(1)}, f32[8,128]{1,0:T(8,128)S(1)}, ...), branch_computations={%region_0.1_spmd, %region_1.0_spmd} | conditional | flops 1576960 | bytes 565272 | solution.py:97
  1.4 2.0 %fusion = f32[8,1,128]{2,1,0:T(1,128)S(1)} fusion(f32[8,128,1]{1,2,0:T(1,128)S(1)} %bitcast.163, f32[1,8,128,128]{3,2,1,0:T(8,128)} %get-tuple-element.299), kind=kOutput, calls=%fused_computation | convolution fusion | flops 1572864 | bytes 532480 | tf_op jit(solution)/shard_map/while/body/eval_jaxpr/cond/branch_1_fun/cij,cj->ci/dot_general | solution.py:36
  3.3 3.7 %collective-permute-start = (f32[8,128]{1,0:T(8,128)S(1)}, f32[8,128]{1,0:T(8,128)S(1)}, u32[]{:S(2)}, u32[]{:S(2)}) collective-permute-start(f32[8,128]{1,0:T(8,128)S(1)} %get-tuple-element.352), channel_id=1, source_target_pairs={{0,16},{1,17},{2,18},{3,19},{4,20},{5,21},{6,22},{7,23},{8,24},{9,... | collective-permute-start | bytes 12296 | tf_op jit(solution)/shard_map/while/body/eval_jaxpr/ppermute | solution.py:32
  9.6 1.3 collective-permute-start.2
  11.0 3.4 %collective-permute-done.2 = f32[1,1,128]{2,1,0:T(1,128)S(1)} collective-permute-done((f32[1,1,128]{2,1,0:T(1,128)S(1)}, f32[1,1,128]{2,1,0:T(1,128)S(1)}, u32[]{:S(2)}, u32[]{:S(2)}) %collective-permute-start.2) | collective-permute-done | bytes 544 | tf_op jit(solution)/shard_map/ppermute | solution.py:22
  14.5 1.3 conditional.10
  15.8 1.3 collective-permute-start.3
  17.1 7.8 %collective-permute-done.3 = f32[8,128]{1,0:T(8,128)S(1)} collective-permute-done((f32[8,128]{1,0:T(8,128)S(1)}, f32[8,128]{1,0:T(8,128)S(1)}, u32[]{:S(2)}, u32[]{:S(2)}) %collective-permute-start.3) | collective-permute-done | bytes 4128 | tf_op jit(solution)/shard_map/while/body/eval_jaxpr/ppermute | solution.py:32
  24.9 2.6 %conditional.11 = (f32[1,8,128]{2,1,0:T(8,128)}) conditional(s32[]{:T(128)} %convert_element_type.20, f32[1,8,128]{2,1,0:T(8,128)} %get-tuple-element.355, (f32[1,8,128]{2,1,0:T(8,128)S(1)}, f32[1,8,128]{2,1,0:T(8,128)S(1)}, f32[8,128]{1,0:T(8,128)S(1)}, f32[8,128]{1,0:T(8,128)S(1)}, f32[1,8,128,128]{3,2,1,0:T(8,128)}) %tuple.139), branch_computations={%region_6.7_spmd, %region_7.0_spmd} | conditional | flops 1576960 | bytes 561160 | solution.py:97
  24.9 2.0 %fusion.6 = f32[8,1,128]{2,1,0:T(1,128)S(1)} fusion(f32[8,128,1]{1,2,0:T(1,128)S(1)} %bitcast.166, f32[1,8,128,128]{3,2,1,0:T(8,128)} %get-tuple-element.313), kind=kOutput, calls=%fused_computation.12 | convolution fusion | flops 1572864 | bytes 532480 | tf_op jit(solution)/shard_map/cond/branch_1_fun/cij,cj->ci/dot_general | solution.py:36
  28.8 1.3 collective-permute-start.5
  30.3 4.2 %collective-permute-done.5 = f32[1,8,128]{2,1,0:T(8,128)S(1)} collective-permute-done((f32[1,8,128]{2,1,0:T(8,128)}, f32[1,8,128]{2,1,0:T(8,128)S(1)}, u32[]{:S(2)}, u32[]{:S(2)}) %collective-permute-start.5) | collective-permute-done | bytes 4128 | tf_op jit(solution)/shard_map/ppermute | solution.py:22
  35.3 2.2 %collective-permute-start.6 = (f32[3,1,128]{2,1,0:T(1,128)S(1)}, f32[3,1,128]{2,1,0:T(1,128)S(1)}, u32[]{:S(2)}, u32[]{:S(2)}) collective-permute-start(f32[3,1,128]{2,1,0:T(1,128)S(1)} %get-tuple-element.382), channel_id=1, source_target_pairs={{0,1},{1,2},{2,3},{3,4},{4,5},{5,6},{6,7},{7,8},{8,9},{9,10},{10,1... | collective-permute-start | bytes 4616 | tf_op jit(solution)/shard_map/ppermute | solution.py:20
  37.5 1.3 collective-permute-start.7
  39.6 2.5 %collective-permute-done.7 = f32[3,1,128]{2,1,0:T(1,128)S(1)} collective-permute-done((f32[3,1,128]{2,1,0:T(1,128)S(1)}, f32[3,1,128]{2,1,0:T(1,128)S(1)}, u32[]{:S(2)}, u32[]{:S(2)}) %collective-permute-start.7) | collective-permute-done | bytes 1568 | tf_op jit(solution)/shard_map/ppermute | solution.py:22
  42.1 1.5 multiply_reduce_fusion.4
  43.7 43.3 %all-reduce.9 = (f32[]{:T(128)}, f32[]{:T(128)}) all-reduce(f32[]{:T(128)} %get-tuple-element.369, f32[]{:T(128)} %get-tuple-element.368), channel_id=1, replica_groups=mesh['wave'=2,'plane'=16] {'wave','plane'}, use_global_device_ids=true, to_apply=%region_9.10 | all-reduce | flops 2 | bytes 16 | tf_op jit(solution)/shard_map/psum | solution.py:146
  88.3 2.0 %conditional.12 = (f32[1,8,128]{2,1,0:T(8,128)S(1)}, f32[8,128]{1,0:T(8,128)S(1)}, f32[8,128]{1,0:T(8,128)S(1)}) conditional(s32[]{:T(128)} %convert_element_type.23, (f32[1,8,128]{2,1,0:T(8,128)}, f32[8,128]{1,0:T(8,128)S(1)}) %tuple.145, (f32[1,8,128]{2,1,0:T(8,128)S(1)}, f32[8,128]{1,0:T(8,128)S(1)}, f32[8,128]{1,0:T(8,128)S(1)}, ...), branch_computations={%region_12.13_spmd, %region_13.14_spmd} | conditional | flops 1576960 | bytes 565272 | solution.py:97
  88.4 2.0 %fusion.9 = f32[8,1,128]{2,1,0:T(1,128)S(1)} fusion(f32[8,128,1]{1,2,0:T(1,128)S(1)} %bitcast.167, f32[1,8,128,128]{3,2,1,0:T(8,128)} %get-tuple-element.319), kind=kOutput, calls=%fused_computation.17 | convolution fusion | flops 1572864 | bytes 532480 | tf_op jit(solution)/shard_map/while/body/eval_jaxpr/cond/branch_1_fun/cij,cj->ci/dot_general | solution.py:36
  90.3 2.9 %collective-permute-start.8 = (f32[8,128]{1,0:T(8,128)S(1)}, f32[8,128]{1,0:T(8,128)S(1)}, u32[]{:S(2)}, u32[]{:S(2)}) collective-permute-start(f32[8,128]{1,0:T(8,128)S(1)} %get-tuple-element.359), channel_id=1, source_target_pairs={{0,16},{1,17},{2,18},{3,19},{4,20},{5,21},{6,22},{7,23},{8,24},{9,... | collective-permute-start | bytes 12296 | tf_op jit(solution)/shard_map/while/body/eval_jaxpr/ppermute | solution.py:32
  93.2 1.3 collective-permute-done.8
  95.8 3.0 %collective-permute-start.9 = (f32[1,1,128]{2,1,0:T(1,128)S(1)}, f32[1,1,128]{2,1,0:T(1,128)S(1)}, u32[]{:S(2)}, u32[]{:S(2)}) collective-permute-start(f32[1,1,128]{2,1,0:T(1,128)S(1)} %get-tuple-element.388), channel_id=1, source_target_pairs={{0,1},{1,2},{2,3},{3,4},{4,5},{5,6},{6,7},{7,8},{8,9},{9,10},{10,1... | collective-permute-start | bytes 1544 | tf_op jit(solution)/shard_map/ppermute | solution.py:20
  101.0 9.1 %collective-permute-done.11 = f32[8,128]{1,0:T(8,128)S(1)} collective-permute-done((f32[8,128]{1,0:T(8,128)S(1)}, f32[8,128]{1,0:T(8,128)S(1)}, u32[]{:S(2)}, u32[]{:S(2)}) %collective-permute-start.11) | collective-permute-done | bytes 4128 | tf_op jit(solution)/shard_map/while/body/eval_jaxpr/ppermute | solution.py:32
  110.1 2.6 %conditional.15 = (f32[1,8,128]{2,1,0:T(8,128)}) conditional(s32[]{:T(128)} %convert_element_type.20, f32[1,8,128]{2,1,0:T(8,128)} %get-tuple-element.362, (f32[1,8,128]{2,1,0:T(8,128)S(1)}, f32[1,8,128]{2,1,0:T(8,128)S(1)}, f32[8,128]{1,0:T(8,128)S(1)}, f32[8,128]{1,0:T(8,128)S(1)}, f32[1,8,128,128]{3,2,1,0:T(8,128)}) %tuple.143), branch_computations={%region_18.0_spmd, %region_19.20_spmd} | conditional | flops 1576960 | bytes 561160 | solution.py:97
  110.2 2.0 %fusion.15 = f32[8,1,128]{2,1,0:T(1,128)S(1)} fusion(f32[8,128,1]{1,2,0:T(1,128)S(1)} %bitcast.170, f32[1,8,128,128]{3,2,1,0:T(8,128)} %get-tuple-element.333), kind=kOutput, calls=%fused_computation.29 | convolution fusion | flops 1572864 | bytes 532480 | tf_op jit(solution)/shard_map/cond/branch_1_fun/cij,cj->ci/dot_general | solution.py:36
  114.0 1.3 collective-permute-start.13
  115.5 4.2 %collective-permute-done.13 = f32[1,8,128]{2,1,0:T(8,128)S(1)} collective-permute-done((f32[1,8,128]{2,1,0:T(8,128)}, f32[1,8,128]{2,1,0:T(8,128)S(1)}, u32[]{:S(2)}, u32[]{:S(2)}) %collective-permute-start.13) | collective-permute-done | bytes 4128 | tf_op jit(solution)/shard_map/ppermute | solution.py:22
  121.8 1.3 collective-permute-start.15
  123.9 3.8 %collective-permute-done.15 = f32[3,1,128]{2,1,0:T(1,128)S(1)} collective-permute-done((f32[3,1,128]{2,1,0:T(1,128)S(1)}, f32[3,1,128]{2,1,0:T(1,128)S(1)}, u32[]{:S(2)}, u32[]{:S(2)}) %collective-permute-start.15) | collective-permute-done | bytes 1568 | tf_op jit(solution)/shard_map/ppermute | solution.py:22
  127.7 1.6 multiply_reduce_fusion
  129.2 42.7 %all-reduce.8 = (f32[]{:T(128)}, f32[]{:T(128)}, f32[]{:T(128)}, f32[]{:T(128)}) all-reduce(f32[]{:T(128)} %get-tuple-element.365, f32[]{:T(128)} %get-tuple-element.366, f32[]{:T(128)} %get-tuple-element.367, f32[]{:T(128)} %get-tuple-element.364), channel_id=1, replica_groups=mesh['wave'=2,'plane'=16] {'wave','plane'}, use_global_device_ids=true, to_apply=%region_23.0 | all-reduce | flops 4 | bytes 32 | tf_op jit(solution)/shard_map/psum | solution.py:146
  176.4 1.3 multiply_subtract_fusion
  (55 shorter events, 16.9 us)
Async XLA Ops:
  0.6 0.7 copy-start.2
  0.7 0.7 copy-start
  3.3 3.7 %copy-start.3 = (f32[1,128]{1,0:T(1,128)S(1)}, f32[1,128]{1,0:T(1,128)}, u32[]{:S(2)}) copy-start(f32[1,128]{1,0:T(1,128)} %param.23) | copy-start | bytes 1540
  3.3 5.0 %collective-permute-start = (f32[8,128]{1,0:T(8,128)S(1)}, f32[8,128]{1,0:T(8,128)S(1)}, u32[]{:S(2)}, u32[]{:S(2)}) collective-permute-start(f32[8,128]{1,0:T(8,128)S(1)} %get-tuple-element.352), channel_id=1, source_target_pairs={{0,16},{1,17},{2,18},{3,19},{4,20},{5,21},{6,22},{7,23},{8,24},{9,... | collective-permute-start | bytes 12296 | tf_op jit(solution)/shard_map/while/body/eval_jaxpr/ppermute | solution.py:32
  7.1 0.7 copy-start.1
  8.4 2.7 %collective-permute-start.1 = (f32[1,1,128]{2,1,0:T(1,128)S(1)}, f32[1,1,128]{2,1,0:T(1,128)S(1)}, u32[]{:S(2)}, u32[]{:S(2)}) collective-permute-start(f32[1,1,128]{2,1,0:T(1,128)S(1)} %get-tuple-element.394), channel_id=1, source_target_pairs={{0,1},{1,2},{2,3},{3,4},{4,5},{5,6},{6,7},{7,8},{8,9},{9,10},{10,1... | collective-permute-start | bytes 1544 | tf_op jit(solution)/shard_map/ppermute | solution.py:20
  9.6 4.8 %collective-permute-start.2 = (f32[1,1,128]{2,1,0:T(1,128)S(1)}, f32[1,1,128]{2,1,0:T(1,128)S(1)}, u32[]{:S(2)}, u32[]{:S(2)}) collective-permute-start(f32[1,1,128]{2,1,0:T(1,128)S(1)} %get-tuple-element.395), channel_id=1, source_target_pairs={{1,0},{2,1},{3,2},{4,3},{5,4},{6,5},{7,6},{8,7},{9,8},{10,9},{11,1... | collective-permute-start | bytes 1544 | tf_op jit(solution)/shard_map/ppermute | solution.py:22
  15.8 9.1 %collective-permute-start.3 = (f32[8,128]{1,0:T(8,128)S(1)}, f32[8,128]{1,0:T(8,128)S(1)}, u32[]{:S(2)}, u32[]{:S(2)}) collective-permute-start(f32[8,128]{1,0:T(8,128)S(1)} %get-tuple-element.356), channel_id=1, source_target_pairs={{16,0},{17,1},{18,2},{19,3},{20,4},{21,5},{22,6},{23,7},{24,8},{25... | collective-permute-start | bytes 12296 | tf_op jit(solution)/shard_map/while/body/eval_jaxpr/ppermute | solution.py:32
  27.5 2.8 %collective-permute-start.4 = (f32[1,8,128]{2,1,0:T(8,128)}, f32[1,8,128]{2,1,0:T(8,128)S(1)}, u32[]{:S(2)}, u32[]{:S(2)}) collective-permute-start(f32[1,8,128]{2,1,0:T(8,128)} %get-tuple-element.426), channel_id=1, source_target_pairs={{0,16},{1,17},{2,18},{3,19},{4,20},{5,21},{6,22},{7,23},{8,24},{9,... | collective-permute-start | bytes 12296 | tf_op jit(solution)/shard_map/ppermute | solution.py:20
  28.8 5.7 %collective-permute-start.5 = (f32[1,8,128]{2,1,0:T(8,128)}, f32[1,8,128]{2,1,0:T(8,128)S(1)}, u32[]{:S(2)}, u32[]{:S(2)}) collective-permute-start(f32[1,8,128]{2,1,0:T(8,128)} %get-tuple-element.426), channel_id=1, source_target_pairs={{16,0},{17,1},{18,2},{19,3},{20,4},{21,5},{22,6},{23,7},{24,8},{25... | collective-permute-start | bytes 12296 | tf_op jit(solution)/shard_map/ppermute | solution.py:22
  35.3 4.4 %collective-permute-start.6 = (f32[3,1,128]{2,1,0:T(1,128)S(1)}, f32[3,1,128]{2,1,0:T(1,128)S(1)}, u32[]{:S(2)}, u32[]{:S(2)}) collective-permute-start(f32[3,1,128]{2,1,0:T(1,128)S(1)} %get-tuple-element.382), channel_id=1, source_target_pairs={{0,1},{1,2},{2,3},{3,4},{4,5},{5,6},{6,7},{7,8},{8,9},{9,10},{10,1... | collective-permute-start | bytes 4616 | tf_op jit(solution)/shard_map/ppermute | solution.py:20
  37.5 4.6 %collective-permute-start.7 = (f32[3,1,128]{2,1,0:T(1,128)S(1)}, f32[3,1,128]{2,1,0:T(1,128)S(1)}, u32[]{:S(2)}, u32[]{:S(2)}) collective-permute-start(f32[3,1,128]{2,1,0:T(1,128)S(1)} %get-tuple-element.383), channel_id=1, source_target_pairs={{1,0},{2,1},{3,2},{4,3},{5,4},{6,5},{7,6},{8,7},{9,8},{10,9},{11,1... | collective-permute-start | bytes 4616 | tf_op jit(solution)/shard_map/ppermute | solution.py:22
  90.3 4.2 %collective-permute-start.8 = (f32[8,128]{1,0:T(8,128)S(1)}, f32[8,128]{1,0:T(8,128)S(1)}, u32[]{:S(2)}, u32[]{:S(2)}) collective-permute-start(f32[8,128]{1,0:T(8,128)S(1)} %get-tuple-element.359), channel_id=1, source_target_pairs={{0,16},{1,17},{2,18},{3,19},{4,20},{5,21},{6,22},{7,23},{8,24},{9,... | collective-permute-start | bytes 12296 | tf_op jit(solution)/shard_map/while/body/eval_jaxpr/ppermute | solution.py:32
  94.5 4.4 %collective-permute-start.10 = (f32[1,1,128]{2,1,0:T(1,128)S(1)}, f32[1,1,128]{2,1,0:T(1,128)S(1)}, u32[]{:S(2)}, u32[]{:S(2)}) collective-permute-start(f32[1,1,128]{2,1,0:T(1,128)S(1)} %get-tuple-element.389), channel_id=1, source_target_pairs={{1,0},{2,1},{3,2},{4,3},{5,4},{6,5},{7,6},{8,7},{9,8},{10,9},{11,1... | collective-permute-start | bytes 1544 | tf_op jit(solution)/shard_map/ppermute | solution.py:22
  95.8 3.8 %collective-permute-start.9 = (f32[1,1,128]{2,1,0:T(1,128)S(1)}, f32[1,1,128]{2,1,0:T(1,128)S(1)}, u32[]{:S(2)}, u32[]{:S(2)}) collective-permute-start(f32[1,1,128]{2,1,0:T(1,128)S(1)} %get-tuple-element.388), channel_id=1, source_target_pairs={{0,1},{1,2},{2,3},{3,4},{4,5},{5,6},{6,7},{7,8},{8,9},{9,10},{10,1... | collective-permute-start | bytes 1544 | tf_op jit(solution)/shard_map/ppermute | solution.py:20
  99.8 10.4 %collective-permute-start.11 = (f32[8,128]{1,0:T(8,128)S(1)}, f32[8,128]{1,0:T(8,128)S(1)}, u32[]{:S(2)}, u32[]{:S(2)}) collective-permute-start(f32[8,128]{1,0:T(8,128)S(1)} %get-tuple-element.363), channel_id=1, source_target_pairs={{16,0},{17,1},{18,2},{19,3},{20,4},{21,5},{22,6},{23,7},{24,8},{25... | collective-permute-start | bytes 12296 | tf_op jit(solution)/shard_map/while/body/eval_jaxpr/ppermute | solution.py:32
  112.7 2.8 %collective-permute-start.12 = (f32[1,8,128]{2,1,0:T(8,128)}, f32[1,8,128]{2,1,0:T(8,128)S(1)}, u32[]{:S(2)}, u32[]{:S(2)}) collective-permute-start(f32[1,8,128]{2,1,0:T(8,128)} %get-tuple-element.427), channel_id=1, source_target_pairs={{0,16},{1,17},{2,18},{3,19},{4,20},{5,21},{6,22},{7,23},{8,24},{9,... | collective-permute-start | bytes 12296 | tf_op jit(solution)/shard_map/ppermute | solution.py:20
  114.0 5.7 %collective-permute-start.13 = (f32[1,8,128]{2,1,0:T(8,128)}, f32[1,8,128]{2,1,0:T(8,128)S(1)}, u32[]{:S(2)}, u32[]{:S(2)}) collective-permute-start(f32[1,8,128]{2,1,0:T(8,128)} %get-tuple-element.427), channel_id=1, source_target_pairs={{16,0},{17,1},{18,2},{19,3},{20,4},{21,5},{22,6},{23,7},{24,8},{25... | collective-permute-start | bytes 12296 | tf_op jit(solution)/shard_map/ppermute | solution.py:22
  120.5 3.4 %collective-permute-start.14 = (f32[3,1,128]{2,1,0:T(1,128)S(1)}, f32[3,1,128]{2,1,0:T(1,128)S(1)}, u32[]{:S(2)}, u32[]{:S(2)}) collective-permute-start(f32[3,1,128]{2,1,0:T(1,128)S(1)} %get-tuple-element.380), channel_id=1, source_target_pairs={{0,1},{1,2},{2,3},{3,4},{4,5},{5,6},{6,7},{7,8},{8,9},{9,10},{10,1... | collective-permute-start | bytes 4616 | tf_op jit(solution)/shard_map/ppermute | solution.py:20
  121.8 5.9 %collective-permute-start.15 = (f32[3,1,128]{2,1,0:T(1,128)S(1)}, f32[3,1,128]{2,1,0:T(1,128)S(1)}, u32[]{:S(2)}, u32[]{:S(2)}) collective-permute-start(f32[3,1,128]{2,1,0:T(1,128)S(1)} %get-tuple-element.381), channel_id=1, source_target_pairs={{1,0},{2,1},{3,2},{4,3},{5,4},{6,5},{7,6},{8,7},{9,8},{10,9},{11,1... | collective-permute-start | bytes 4616 | tf_op jit(solution)/shard_map/ppermute | solution.py:22
where the time goes:
time: 179 us; the launch traced here: 178 us
  blocking collectives  86 us (48%)
  waiting for transfers between devices  38 us (21%)
  starting transfers between devices  27.2 us (15%)
  matrix products  7.82 us (4%)
  other arithmetic  7.38 us (4%)
  between operations  6.7 us (4%)
  local copies, waits for them, and re-layouts  4.56 us (3%)
    psum x2, blocking collectives, on_device(): lax.psum((across_term, jnp.sum(precond * residual), older_term, jnp.sum(p...  86 us
    ppermute x4, waiting for transfers between devices, passed_along(): return lax.ppermute(block, axis, route)  18.7 us
    ppermute x6, waiting for transfers between devices, extended(): lax.ppermute(head, axis, [((i + 1) % count, i) for i in range(ends)])  18.1 us
    ppermute x6, starting transfers between devices, extended(): lax.ppermute(tail, axis, [(i, (i + 1) % count) for i in range(ends)])  10.3 us
    ppermute x4, starting transfers between devices, passed_along(): return lax.ppermute(block, axis, route)  9.13 us
    dot_general x4, matrix products, apply_block(): jnp.einsum('cij,cj->ci', block, vector, precision=lax.Precision.HIGHEST)  7.82 us
    ppermute x6, starting transfers between devices, extended(): lax.ppermute(head, axis, [((i + 1) % count, i) for i in range(ends)])  7.74 us
  transfers between devices with their start and end apart: 16, of which 12 were waited for; matrix products, arithmetic and copies ran while one was open for 1% of the time, Pallas kernels for 0%

commit v1 on v0

v1 whole, which is shorter than its diff:
```python
import functools

import jax
import jax.numpy as jnp
from jax import lax
from jax.experimental import pallas as pl
from jax.experimental.pallas import tpu as pltpu
from jax.sharding import PartitionSpec as P

relax = 1.5
MESH = pl.DeviceIdType.MESH
DIRECT = 64


def kernel(
    sections, strips,
    right_ref, cx_ref, cy_ref, cz_ref, inverse_ref,
    solution_ref, residual_ref,
    block, weights, half, field, half_edge, field_edge,
    from_lower_half, from_upper, from_lower, half_halo, field_halo,
    sums, gathered,
    load_sem, send_x, recv_x, send_y, recv_y, send_sum, recv_sum,
):
    depth, columns, cells = right_ref.shape
    w = lax.axis_index("wave")
    p = lax.axis_index("plane")
    devices = sections * strips

    load = pltpu.make_async_copy(inverse_ref, block, load_sem)
    load.start()

    barrier = pltpu.get_barrier_semaphore()
    single = devices <= DIRECT
    if single:
        groups = [(devices, w * strips + p, lambda t: (t // strips, t % strips))]
    else:
        groups = [(sections, w, lambda t: (t, p)), (strips, p, lambda t: (w, t))]
    greeted = 0
    for count, me, where in groups:
        for offset in range(1, count):
            pl.semaphore_signal(
                barrier, inc=1, device_id=where((me + offset) % count), device_id_type=MESH
            )
        greeted += count - 1

    lane = lax.broadcasted_iota(jnp.int32, (columns, cells), 1)
    row = lax.broadcasted_iota(jnp.int32, (columns, cells), 0)
    cx = cx_ref[...]
    cy, lower_z, upper_z, centre = [], [], [], []
    for d in range(depth):
        cz = cz_ref[d]
        above = pltpu.roll(cz, cells - 1, 1)
        cy.append(jnp.broadcast_to(cy_ref[d : d + 1, :], (columns, cells)))
        centre.append(2.0 * cx + 2.0 * cy[d] + cz + above)
        lower_z.append(jnp.where(lane == 0, 0.0, cz))
        upper_z.append(jnp.where(lane == cells - 1, 0.0, above))

    nothing = jnp.zeros((columns, cells), jnp.float32)
    no_edge = jnp.zeros((depth, 1, cells), jnp.float32)

    @pl.when(w == 0)
    def _():
        for k in range(2):
            from_lower_half[k] = nothing
            from_lower[k] = nothing

    @pl.when(w == sections - 1)
    def _():
        for k in range(2):
            from_upper[k] = nothing

    @pl.when(p == 0)
    def _():
        for k in range(2):
            half_halo[k, 0] = no_edge
            field_halo[k, 0] = no_edge

    @pl.when(p == strips - 1)
    def _():
        for k in range(2):
            half_halo[k, 1] = no_edge
            field_halo[k, 1] = no_edge

    load.wait()
    for d in range(depth):
        for c in range(columns):
            weights[d, pl.ds(c, cells, stride=columns), :] = block[d, c].T

    def apply_block(d, v):
        parts = [None] * 4
        for j in range(cells):
            term = weights[d, pl.ds(j * columns, columns), :] * jnp.broadcast_to(
                v[:, j : j + 1], (columns, cells)
            )
            parts[j % 4] = term if parts[j % 4] is None else parts[j % 4] + term
        return relax * ((parts[0] + parts[1]) + (parts[2] + parts[3]))

    def column_part(d, v):
        return (
            centre[d] * v
            - lower_z[d] * pltpu.roll(v, 1, 1)
            - upper_z[d] * pltpu.roll(v, cells - 1, 1)
        )

    def along_y(v, low, high):
        below = jnp.where(row == 0, low, pltpu.roll(v, 1, 0))
        above = jnp.where(row == columns - 1, high, pltpu.roll(v, columns - 1, 0))
        return below + above

    def x_copy(source, target, slot, step):
        return pltpu.make_async_remote_copy(
            src_ref=source, dst_ref=target, send_sem=send_x.at[slot], recv_sem=recv_x.at[slot],
            device_id=(w + step, p), device_id_type=MESH,
        )

    def y_copy(edges, halo, k, side, slot):
        return pltpu.make_async_remote_copy(
            src_ref=edges.at[k, side], dst_ref=halo.at[k, 1 - side],
            send_sem=send_y.at[slot + side], recv_sem=recv_y.at[slot + side],
            device_id=(w, p + (2 * side - 1)), device_id_type=MESH,
        )

    def send_edges(planes, edges, halo, k, slot):
        for d in range(depth):
            edges[k, 0, d] = planes[d][:1]
            edges[k, 1, d] = planes[d][columns - 1 :]

        @pl.when(p > 0)
        def _():
            y_copy(edges, halo, k, 0, slot).start()

        @pl.when(p < strips - 1)
        def _():
            y_copy(edges, halo, k, 1, slot).start()

    def wait_edges(edges, halo, k, slot):
        @pl.when(p > 0)
        def _():
            y_copy(edges, halo, k, 1, slot).wait_recv()

        @pl.when(p < strips - 1)
        def _():
            y_copy(edges, halo, k, 0, slot).wait_recv()

    def wait_sent(edges, halo, k, slot):
        @pl.when(p > 0)
        def _():
            y_copy(edges, halo, k, 0, slot).wait_send()

        @pl.when(p < strips - 1)
        def _():
            y_copy(edges, halo, k, 1, slot).wait_send()

    def precondition(source, k, first):
        slot = 3 * k
        edge_slot = 4 * k
        up_half = x_copy(half.at[k, depth - 1], from_lower_half.at[k], slot, 1)
        down_field = x_copy(field.at[k, 0], from_upper.at[k], slot + 1, -1)
        up_field = x_copy(field.at[k, depth - 1], from_lower.at[k], slot + 2, 1)

        if first:
            pl.semaphore_wait(barrier, greeted)

        @pl.when(w > 0)
        def _():
            up_half.wait_recv()

        lower = [from_lower_half[k]]
        h = []
        for d in range(depth):
            h.append(apply_block(d, source[d] + cx * lower[d]))
            lower.append(h[d])
            half[k, d] = h[d]

        @pl.when(w < sections - 1)
        def _():
            up_half.start()

        send_edges(h, half_edge, half_halo, k, edge_slot)
        partial = [source[d] - (column_part(d, h[d]) - cx * lower[d]) for d in range(depth)]
        wait_edges(half_edge, half_halo, k, edge_slot)
        rest = [
            partial[d] + cy[d] * along_y(h[d], half_halo[k, 0, d], half_halo[k, 1, d])
            for d in range(depth)
        ]

        @pl.when(w < sections - 1)
        def _():
            down_field.wait_recv()

        upper = from_upper[k]
        z = [None] * depth
        above = [None] * depth
        previous = upper
        for d in reversed(range(depth)):
            above[d] = previous
            z[d] = h[d] + apply_block(d, rest[d] + cx * previous)
            previous = z[d]
            field[k, d] = z[d]

        @pl.when(w > 0)
        def _():
            down_field.start()

        @pl.when(w < sections - 1)
        def _():
            up_field.start()

        send_edges(z, field_edge, field_halo, k, edge_slot + 2)
        partial = [column_part(d, z[d]) for d in range(depth)]
        wait_edges(field_edge, field_halo, k, edge_slot + 2)

        @pl.when(w > 0)
        def _():
            up_field.wait_recv()

        below = from_lower[k]
        image = []
        for d in range(depth):
            image.append(
                partial[d]
                - cx * (below + above[d])
                - cy[d] * along_y(z[d], field_halo[k, 0, d], field_halo[k, 1, d])
            )
            below = z[d]
        return z, image

    def finish(k):
        slot = 3 * k
        edge_slot = 4 * k

        @pl.when(w < sections - 1)
        def _():
            x_copy(half.at[k, depth - 1], from_lower_half.at[k], slot, 1).wait_send()
            x_copy(field.at[k, depth - 1], from_lower.at[k], slot + 2, 1).wait_send()

        @pl.when(w > 0)
        def _():
            x_copy(field.at[k, 0], from_upper.at[k], slot + 1, -1).wait_send()

        wait_sent(half_edge, half_halo, k, edge_slot)
        wait_sent(field_edge, field_halo, k, edge_slot + 2)

    right = [right_ref[d] for d in range(depth)]
    z, q = precondition(right, 0, True)
    y, u = precondition(q, 1, False)

    def inner(a, b):
        total = a[0] * b[0]
        for d in range(1, depth):
            total = total + a[d] * b[d]
        return jnp.sum(jnp.sum(total, axis=0, keepdims=True), axis=1, keepdims=True)

    spot = lax.broadcasted_iota(jnp.int32, (1, cells), 1)
    packed = jnp.zeros((1, cells), jnp.float32)
    pairs = [(z, right), (z, q), (y, q), (y, right), (y, u), (z, u)]
    for i, (a, b) in enumerate(pairs):
        packed = jnp.where(spot == i, inner(a, b), packed)

    base = 0
    for stage, (count, me, where) in enumerate(groups):
        sums[stage] = packed
        gathered[base + me] = packed

        def send(offset):
            return pltpu.make_async_remote_copy(
                src_ref=sums.at[stage], dst_ref=gathered.at[base + me],
                send_sem=send_sum.at[base + offset], recv_sem=recv_sum.at[base + me],
                device_id=where((me + offset) % count), device_id_type=MESH,
            )

        def arrival(sender):
            return pltpu.make_async_remote_copy(
                src_ref=sums.at[stage], dst_ref=gathered.at[base + sender],
                send_sem=send_sum.at[base], recv_sem=recv_sum.at[base + sender],
                device_id=where(sender), device_id_type=MESH,
            )

        for offset in range(1, count):
            send(offset).start()
        if stage == 0:
            finish(0)
            finish(1)
        for offset in range(1, count):
            arrival((me + offset) % count).wait_recv()
        parts = [gathered[base + i] for i in range(count)]
        while len(parts) > 1:
            parts = [
                parts[i] + parts[i + 1] if i + 1 < len(parts) else parts[i]
                for i in range(0, len(parts), 2)
            ]
        packed = parts[0]
        for offset in range(1, count):
            send(offset).wait_send()
        base += count

    zr, zq, yq, yr, yu, zu = [
        jnp.broadcast_to(packed[:, i : i + 1], (1, cells)) for i in range(len(pairs))
    ]
    first_step = zr / zq
    keep = 1.0 - (zq - first_step * yq) / zq
    projection = keep * (zr - first_step * zq) - first_step * (yr - first_step * yq)
    curvature = (
        keep * keep * zq - keep * first_step * (yq + zu) + first_step * first_step * yu
    )
    step = projection / curvature
    of_z = first_step + step * keep
    of_y = step * first_step
    for d in range(depth):
        solution_ref[d] = of_z * z[d] - of_y * y[d]
        residual_ref[d] = right[d] - of_z * q[d] + of_y * u[d]


def solution(mesh):
    sections = mesh.shape["wave"]
    strips = mesh.shape["plane"]

    def on_device(right_side, coupling_x, coupling_y, coupling_z, inverse):
        depth, columns, cells = right_side.shape
        devices = sections * strips
        slots = devices if devices <= DIRECT else sections + strips
        vmem = pl.BlockSpec(memory_space=pltpu.VMEM)
        plane = (columns, cells)
        out = jax.ShapeDtypeStruct(right_side.shape, jnp.float32)
        return pl.pallas_call(
            functools.partial(kernel, sections, strips),
            out_shape=(out, out),
            in_specs=[vmem] * 4 + [pl.BlockSpec(memory_space=pl.ANY)],
            out_specs=(vmem, vmem),
            scratch_shapes=[
                pltpu.VMEM(inverse.shape, jnp.float32),
                pltpu.VMEM((depth, cells * columns, cells), jnp.float32),
                pltpu.VMEM((2, depth) + plane, jnp.float32),
                pltpu.VMEM((2, depth) + plane, jnp.float32),
                pltpu.VMEM((2, 2, depth, 1, cells), jnp.float32),
                pltpu.VMEM((2, 2, depth, 1, cells), jnp.float32),
                pltpu.VMEM((2,) + plane, jnp.float32),
                pltpu.VMEM((2,) + plane, jnp.float32),
                pltpu.VMEM((2,) + plane, jnp.float32),
                pltpu.VMEM((2, 2, depth, 1, cells), jnp.float32),
                pltpu.VMEM((2, 2, depth, 1, cells), jnp.float32),
                pltpu.VMEM((2, 1, cells), jnp.float32),
                pltpu.VMEM((slots, 1, cells), jnp.float32),
                pltpu.SemaphoreType.DMA,
                pltpu.SemaphoreType.DMA((6,)),
                pltpu.SemaphoreType.DMA((6,)),
                pltpu.SemaphoreType.DMA((8,)),
                pltpu.SemaphoreType.DMA((8,)),
                pltpu.SemaphoreType.DMA((slots,)),
                pltpu.SemaphoreType.DMA((slots,)),
            ],
            compiler_params=pltpu.CompilerParams(collective_id=0, has_side_effects=True),
        )(right_side, coupling_x, coupling_y, coupling_z, inverse)

    placed = (
        P("wave", "plane", None),
        P("plane", None),
        P("wave", None),
        P("wave", "plane", None),
        P("wave", "plane", None, None),
    )
    return jax.shard_map(
        on_device,
        mesh=mesh,
        in_specs=placed,
        out_specs=(P("wave", "plane", None), P("wave", "plane", None)),
        check_vma=False,
    )
```

time: 179 us -> 36.1 us (0.20)
  blocking collectives: 86 us -> 0 us
  waiting for transfers between devices: 38 us -> 0 us
  Pallas kernels: 0 us -> 33.3 us
  starting transfers between devices: 27.2 us -> 0 us
  matrix products: 7.82 us -> 0 us
  other arithmetic: 7.38 us -> 0 us
  between operations: 6.7 us -> 0.65 us
  local copies, waits for them, and re-layouts: 4.56 us -> 1.86 us
    psum x2 -> x0, blocking collectives: 86 us -> none  [on_device(): lax.psum((across_term, jnp.sum(precond * residual), older_term, jnp.sum(p...]
    ppermute x16 -> x0, waiting for transfers between devices: 38 us -> none  [the longest x4 18.7 us: passed_along(): return lax.ppermute(block, axis, route)]
    pallas_call x0 -> x1, Pallas kernels: none -> 33.3 us  [on_device(): pl.pallas_call(functools.partial(kernel, sections, strips), out_shape=(ou...]
    ppermute x16 -> x0, starting transfers between devices: 27.2 us -> none  [the longest x6 10.3 us: extended(): lax.ppermute(tail, axis, [(i, (i + 1) % count) for i in range(ends)])]
    dot_general x4 -> x0, matrix products: 7.82 us -> none  [apply_block(): jnp.einsum('cij,cj->ci', block, vector, precision=lax.Precision.HIGHEST)]
    reduce_sum x2 -> x0, other arithmetic: 3.1 us -> none  [on_device(): jnp.sum(precond * applied)]
    slice x7 -> x0, local copies, waits for them, and re-layouts: 1.9 us -> none  [the longest x4 1.82 us: column_part(): values[..., :-1]]
  transfers between devices with their start and end apart: 16 -> 0, of which waited for: 12 -> 0; matrix products, arithmetic and copies ran while one was open for 1% -> 0% of each run, Pallas kernels for 0% -> 0%
where the time goes in v1:
time: 36.1 us; the launch traced here: 35.8 us
  Pallas kernels  33.3 us (92%)
  local copies, waits for them, and re-layouts  1.86 us (5%)
  between operations  0.65 us (2%)
    pallas_call x1, Pallas kernels, on_device(): pl.pallas_call(functools.partial(kernel, sections, strips), out_shape=(ou...  33.3 us
    unnamed x4, local copies, waits for them, and re-layouts  1.86 us

profile of v1, /device:TPU:0, one launch (start us, length us, event | category | flops | bytes accessed | tf_op | source)
XLA Modules:
  0.0 35.8 jit_solution(12639702292863621878)
XLA Ops:
  0.6 33.3 %shard_map.68 = (f32[1,8,128]{2,1,0:T(8,128)}, f32[1,8,128]{2,1,0:T(8,128)}) custom-call(f32[1,8,128]{2,1,0:T(8,128)} %right_ref.1, f32[8,128]{1,0:T(8,128)} %cx_ref.1, f32[1,128]{1,0:T(1,128)} %cy_ref.1, f32[1,8,128]{2,1,0:T(8,128)} %cz_ref.1, f32[1,8,128,128]{3,2,1,0:T(8,128)} %inverse_ref.1), custom_call_target="tpu_custom_call" | custom-call | tf_op jit(solution)/shard_map/pallas_call | solution.py:325
  34.0 0.0 copy-start
  34.0 1.3 %copy.9 = f32[1,8,128]{2,1,0:T(8,128)} copy(f32[1,8,128]{2,1,0:T(8,128)} %get-tuple-element.4) | data formatting | bytes 8192
  35.2 0.0 copy-done
  35.2 0.6 %copy.10 = f32[1,8,128]{2,1,0:T(8,128)} copy(f32[1,8,128]{2,1,0:T(8,128)S(1)} %copy-done) | data formatting | bytes 8192
Async XLA Ops:
  34.0 1.3 %copy-start = (f32[1,8,128]{2,1,0:T(8,128)S(1)}, f32[1,8,128]{2,1,0:T(8,128)}, u32[]{:S(2)}) copy-start(f32[1,8,128]{2,1,0:T(8,128)} %get-tuple-element.5) | copy-start | bytes 12292

commit v2 on v1

--- a/solution.py
+++ b/solution.py
@@ -14,9 +14,9 @@
 
 def kernel(
     sections, strips,
-    right_ref, cx_ref, cy_ref, cz_ref, inverse_ref,
+    right_any, cx_any, cy_any, cz_any, inverse_any,
     solution_ref, residual_ref,
-    block, weights, half, field, half_edge, field_edge,
+    right_ref, cx_ref, cy_ref, cz_ref, block, weights, half, field, half_edge, field_edge,
     from_lower_half, from_upper, from_lower, half_halo, field_halo,
     sums, gathered,
     load_sem, send_x, recv_x, send_y, recv_y, send_sum, recv_sum,
@@ -26,15 +26,12 @@
     p = lax.axis_index("plane")
     devices = sections * strips
 
-    load = pltpu.make_async_copy(inverse_ref, block, load_sem)
-    load.start()
-
     barrier = pltpu.get_barrier_semaphore()
     single = devices <= DIRECT
     if single:
         groups = [(devices, w * strips + p, lambda t: (t // strips, t % strips))]
     else:
-        groups = [(sections, w, lambda t: (t, p)), (strips, p, lambda t: (w, t))]
+        groups = [(strips, p, lambda t: (w, t)), (sections, w, lambda t: (t, p))]
     greeted = 0
     for count, me, where in groups:
         for offset in range(1, count):
@@ -42,6 +39,20 @@
                 barrier, inc=1, device_id=where((me + offset) % count), device_id_type=MESH
             )
         greeted += count - 1
+
+    loads = [
+        pltpu.make_async_copy(source, target, load_sem.at[i])
+        for i, (source, target) in enumerate(
+            [
+                (inverse_any, block), (cz_any, cz_ref), (cx_any, cx_ref),
+                (cy_any, cy_ref), (right_any, right_ref),
+            ]
+        )
+    ]
+    for load in loads:
+        load.start()
+    for load in loads[1:]:
+        load.wait()
 
     lane = lax.broadcasted_iota(jnp.int32, (columns, cells), 1)
     row = lax.broadcasted_iota(jnp.int32, (columns, cells), 0)
@@ -81,7 +92,7 @@
             half_halo[k, 1] = no_edge
             field_halo[k, 1] = no_edge
 
-    load.wait()
+    loads[0].wait()
     for d in range(depth):
         for c in range(columns):
             weights[d, pl.ds(c, cells, stride=columns), :] = block[d, c].T
@@ -151,15 +162,12 @@
         def _():
             y_copy(edges, halo, k, 1, slot).wait_send()
 
-    def precondition(source, k, first):
+    def precondition(source, k, meanwhile):
         slot = 3 * k
         edge_slot = 4 * k
         up_half = x_copy(half.at[k, depth - 1], from_lower_half.at[k], slot, 1)
         down_field = x_copy(field.at[k, 0], from_upper.at[k], slot + 1, -1)
         up_field = x_copy(field.at[k, depth - 1], from_lower.at[k], slot + 2, 1)
-
-        if first:
-            pl.semaphore_wait(barrier, greeted)
 
         @pl.when(w > 0)
         def _():
@@ -172,11 +180,15 @@
             lower.append(h[d])
             half[k, d] = h[d]
 
+        if k == 0:
+            pl.semaphore_wait(barrier, greeted)
+
         @pl.when(w < sections - 1)
         def _():
             up_half.start()
 
         send_edges(h, half_edge, half_halo, k, edge_slot)
+        meanwhile()
         partial = [source[d] - (column_part(d, h[d]) - cx * lower[d]) for d in range(depth)]
         wait_edges(half_edge, half_halo, k, edge_slot)
         rest = [
@@ -207,12 +219,15 @@
             up_field.start()
 
         send_edges(z, field_edge, field_halo, k, edge_slot + 2)
-        partial = [column_part(d, z[d]) for d in range(depth)]
+        return z, above, [column_part(d, z[d]) for d in range(depth)]
+
+    def operate(k, z, above, partial):
+        edge_slot = 4 * k
         wait_edges(field_edge, field_halo, k, edge_slot + 2)
 
         @pl.when(w > 0)
         def _():
-            up_field.wait_recv()
+            x_copy(field.at[k, depth - 1], from_lower.at[k], 3 * k + 2, 1).wait_recv()
 
         below = from_lower[k]
         image = []
@@ -223,7 +238,7 @@
                 - cy[d] * along_y(z[d], field_halo[k, 0, d], field_halo[k, 1, d])
             )
             below = z[d]
-        return z, image
+        return image
 
     def finish(k):
         slot = 3 * k
@@ -240,10 +255,6 @@
 
         wait_sent(half_edge, half_halo, k, edge_slot)
         wait_sent(field_edge, field_halo, k, edge_slot + 2)
-
-    right = [right_ref[d] for d in range(depth)]
-    z, q = precondition(right, 0, True)
-    y, u = precondition(q, 1, False)
 
     def inner(a, b):
         total = a[0] * b[0]
@@ -252,56 +263,89 @@
         return jnp.sum(jnp.sum(total, axis=0, keepdims=True), axis=1, keepdims=True)
 
     spot = lax.broadcasted_iota(jnp.int32, (1, cells), 1)
-    packed = jnp.zeros((1, cells), jnp.float32)
-    pairs = [(z, right), (z, q), (y, q), (y, right), (y, u), (z, u)]
-    for i, (a, b) in enumerate(pairs):
-        packed = jnp.where(spot == i, inner(a, b), packed)
+    rows = 1 + 2 * depth
+    right = [right_ref[d] for d in range(depth)]
+    z, above, partial = precondition(right, 0, lambda: None)
+    q = operate(0, z, above, partial)
+
+    def early():
+        sums[0, 0] = jnp.where(
+            spot == 0, inner(z, right), jnp.where(spot == 1, inner(z, q), 0.0)
+        )
+
+    y, above, partial = precondition(q, 1, early)
+    faced = []
+    for d in range(depth):
+        next_column = jnp.where(row == columns - 1, 0.0, pltpu.roll(y[d], columns - 1, 0))
+        faced.append(partial[d] - 2.0 * (cx * above[d] + cy[d] * next_column))
+        sums[0, 1 + 2 * d] = y[d][:1]
+        sums[0, 2 + 2 * d] = cy[d][:1] * y[d][columns - 1 :]
+    packed = sums[0, 0]
+    for i, (a, b) in enumerate([(y, q), (y, right), (y, faced)]):
+        packed = jnp.where(spot == 2 + i, inner(a, b), packed)
 
     base = 0
     for stage, (count, me, where) in enumerate(groups):
-        sums[stage] = packed
-        gathered[base + me] = packed
+        width = rows if stage == 0 else 1
+        sums[stage, 0] = packed
 
         def send(offset):
             return pltpu.make_async_remote_copy(
-                src_ref=sums.at[stage], dst_ref=gathered.at[base + me],
+                src_ref=sums.at[stage, pl.ds(0, width)],
+                dst_ref=gathered.at[base + me, pl.ds(0, width)],
                 send_sem=send_sum.at[base + offset], recv_sem=recv_sum.at[base + me],
                 device_id=where((me + offset) % count), device_id_type=MESH,
             )
 
         def arrival(sender):
             return pltpu.make_async_remote_copy(
-                src_ref=sums.at[stage], dst_ref=gathered.at[base + sender],
+                src_ref=sums.at[stage, pl.ds(0, width)],
+                dst_ref=gathered.at[base + sender, pl.ds(0, width)],
                 send_sem=send_sum.at[base], recv_sem=recv_sum.at[base + sender],
                 device_id=where(sender), device_id_type=MESH,
             )
 
         for offset in range(1, count):
             send(offset).start()
+        for i in range(width):
+            gathered[base + me, i] = sums[stage, i]
         if stage == 0:
+            u = operate(1, y, above, partial)
             finish(0)
             finish(1)
         for offset in range(1, count):
             arrival((me + offset) % count).wait_recv()
-        parts = [gathered[base + i] for i in range(count)]
-        while len(parts) > 1:
-            parts = [
-                parts[i] + parts[i + 1] if i + 1 < len(parts) else parts[i]
-                for i in range(0, len(parts), 2)
-            ]
-        packed = parts[0]
+
+        def tree(parts):
+            while len(parts) > 1:
+                parts = [
+                    parts[i] + parts[i + 1] if i + 1 < len(parts) else parts[i]
+                    for i in range(0, len(parts), 2)
+                ]
+            return parts[0]
+
+        packed = tree([gathered[base + i, 0] for i in range(count)])
+        faces = [
+            gathered[base + i, 2 + 2 * d] * gathered[base + i + 1, 1 + 2 * d]
+            for i in range(count)
+            if stage == 0 and i % strips != strips - 1
+            for d in range(depth)
+        ]
+        if faces:
+            across = jnp.sum(tree(faces), axis=1, keepdims=True)
+            packed = jnp.where(spot == 4, packed - 2.0 * across, packed)
         for offset in range(1, count):
             send(offset).wait_send()
         base += count
 
-    zr, zq, yq, yr, yu, zu = [
-        jnp.broadcast_to(packed[:, i : i + 1], (1, cells)) for i in range(len(pairs))
+    zr, zq, yq, yr, yu = [
+        jnp.broadcast_to(packed[:, i : i + 1], (1, cells)) for i in range(5)
     ]
     first_step = zr / zq
     keep = 1.0 - (zq - first_step * yq) / zq
     projection = keep * (zr - first_step * zq) - first_step * (yr - first_step * yq)
     curvature = (
-        keep * keep * zq - keep * first_step * (yq + zu) + first_step * first_step * yu
+        keep * keep * zq - keep * 2.0 * first_step * yq + first_step * first_step * yu
     )
     step = projection / curvature
     of_z = first_step + step * keep
@@ -321,13 +365,18 @@
         slots = devices if devices <= DIRECT else sections + strips
         vmem = pl.BlockSpec(memory_space=pltpu.VMEM)
         plane = (columns, cells)
-        out = jax.ShapeDtypeStruct(right_side.shape, jnp.float32)
+        out = pltpu.VMEM(right_side.shape, jnp.float32)
+        rows = 1 + 2 * depth
         return pl.pallas_call(
             functools.partial(kernel, sections, strips),
             out_shape=(out, out),
-            in_specs=[vmem] * 4 + [pl.BlockSpec(memory_space=pl.ANY)],
+            in_specs=[pl.BlockSpec(memory_space=pl.ANY)] * 5,
             out_specs=(vmem, vmem),
             scratch_shapes=[
+                pltpu.VMEM(right_side.shape, jnp.float32),
+                pltpu.VMEM(coupling_x.shape, jnp.float32),
+                pltpu.VMEM(coupling_y.shape, jnp.float32),
+                pltpu.VMEM(coupling_z.shape, jnp.float32),
                 pltpu.VMEM(inverse.shape, jnp.float32),
                 pltpu.VMEM((depth, cells * columns, cells), jnp.float32),
                 pltpu.VMEM((2, depth) + plane, jnp.float32),
@@ -339,9 +388,9 @@
                 pltpu.VMEM((2,) + plane, jnp.float32),
                 pltpu.VMEM((2, 2, depth, 1, cells), jnp.float32),
                 pltpu.VMEM((2, 2, depth, 1, cells), jnp.float32),
-                pltpu.VMEM((2, 1, cells), jnp.float32),
-                pltpu.VMEM((slots, 1, cells), jnp.float32),
-                pltpu.SemaphoreType.DMA,
+                pltpu.VMEM((2, rows, 1, cells), jnp.float32),
+                pltpu.VMEM((slots, rows, 1, cells), jnp.float32),
+                pltpu.SemaphoreType.DMA((5,)),
                 pltpu.SemaphoreType.DMA((6,)),
                 pltpu.SemaphoreType.DMA((6,)),
                 pltpu.SemaphoreType.DMA((8,)),

time: 36.1 us -> 31.3 us (0.87)
  Pallas kernels: 33.3 us -> 29.3 us
  local copies, waits for them, and re-layouts: 1.86 us -> 1.19 us
    pallas_call x1, Pallas kernels: 33.3 us -> 29.3 us  [on_device(): pl.pallas_call(functools.partial(kernel, sections, strips), out_shape=(ou...]
    unnamed x4 -> x2, local copies, waits for them, and re-layouts: 1.86 us -> 1.19 us
where the time goes in v2:
time: 31.3 us; the launch traced here: 31.1 us
  Pallas kernels  29.3 us (94%)
  local copies, waits for them, and re-layouts  1.19 us (4%)
  between operations  0.64 us (2%)
    pallas_call x1, Pallas kernels, on_device(): pl.pallas_call(functools.partial(kernel, sections, strips), out_shape=(ou...  29.3 us
    unnamed x2, local copies, waits for them, and re-layouts  1.19 us

profile of v2, /device:TPU:0, one launch (start us, length us, event | category | flops | bytes accessed | tf_op | source)
XLA Modules:
  0.0 31.1 jit_solution(11463013123459132191)
XLA Ops:
  0.6 29.3 %shard_map.68 = (f32[1,8,128]{2,1,0:T(8,128)S(1)}, f32[1,8,128]{2,1,0:T(8,128)S(1)}) custom-call(f32[1,8,128]{2,1,0:T(8,128)} %right_any.1, f32[8,128]{1,0:T(8,128)} %cx_any.1, f32[1,128]{1,0:T(1,128)} %cy_any.1, f32[1,8,128]{2,1,0:T(8,128)} %cz_any.1, f32[1,8,128,128]{3,2,1,0:T(8,128)} %inverse_any.1), custom_call_target="tpu_custom_call" | custom-call | tf_op jit(solution)/shard_map/pallas_call | solution.py:370
  29.9 0.6 %copy.9 = f32[1,8,128]{2,1,0:T(8,128)} copy(f32[1,8,128]{2,1,0:T(8,128)S(1)} %get-tuple-element.2) | data formatting | bytes 8192
  30.5 0.6 %copy.10 = f32[1,8,128]{2,1,0:T(8,128)} copy(f32[1,8,128]{2,1,0:T(8,128)S(1)} %get-tuple-element.3) | data formatting | bytes 8192

commit v3 on v2

--- a/solution.py
+++ b/solution.py
@@ -10,6 +10,7 @@
 relax = 1.5
 MESH = pl.DeviceIdType.MESH
 DIRECT = 64
+RIM_FIRST = False
 
 
 def kernel(
@@ -18,8 +19,10 @@
     solution_ref, residual_ref,
     right_ref, cx_ref, cy_ref, cz_ref, block, weights, half, field, half_edge, field_edge,
     from_lower_half, from_upper, from_lower, half_halo, field_halo,
+    still_edge, still_rim, block_rim, weights_rim, half_rim, field_rim,
+    lower_half_rim, upper_field_rim, lower_field_rim,
     sums, gathered,
-    load_sem, send_x, recv_x, send_y, recv_y, send_sum, recv_sum,
+    load_sem, send_x, recv_x, send_y, recv_y, send_d, recv_d, send_still, recv_still, send_sum, recv_sum,
 ):
     depth, columns, cells = right_ref.shape
     w = lax.axis_index("wave")
@@ -39,6 +42,19 @@
                 barrier, inc=1, device_id=where((me + offset) % count), device_id_type=MESH
             )
         greeted += count - 1
+    if not single:
+        for a in (-1, 1):
+            for b in (-1, 1):
+                near = (
+                    (w + a >= 0) & (w + a < sections) & (p + b >= 0) & (p + b < strips)
+                )
+                greeted = greeted + near.astype(jnp.int32)
+
+                @pl.when(near)
+                def _():
+                    pl.semaphore_signal(
+                        barrier, inc=1, device_id=(w + a, p + b), device_id_type=MESH
+                    )
 
     loads = [
         pltpu.make_async_copy(source, target, load_sem.at[i])
@@ -67,30 +83,42 @@
         upper_z.append(jnp.where(lane == cells - 1, 0.0, above))
 
     nothing = jnp.zeros((columns, cells), jnp.float32)
-    no_edge = jnp.zeros((depth, 1, cells), jnp.float32)
+    no_edge = jnp.zeros((2 * depth, 1, cells), jnp.float32)
+    no_row = jnp.zeros((1, cells), jnp.float32)
+    both_rows = jnp.zeros((2, 1, cells), jnp.float32)
 
     @pl.when(w == 0)
     def _():
         for k in range(2):
             from_lower_half[k] = nothing
             from_lower[k] = nothing
+            lower_half_rim[k] = both_rows
+        lower_field_rim[...] = both_rows
 
     @pl.when(w == sections - 1)
     def _():
         for k in range(2):
             from_upper[k] = nothing
-
-    @pl.when(p == 0)
-    def _():
-        for k in range(2):
-            half_halo[k, 0] = no_edge
-            field_halo[k, 0] = no_edge
-
-    @pl.when(p == strips - 1)
-    def _():
-        for k in range(2):
-            half_halo[k, 1] = no_edge
-            field_halo[k, 1] = no_edge
+        upper_field_rim[...] = both_rows
+
+    for side, last in ((0, 0), (1, strips - 1)):
+
+        @pl.when(p == last)
+        def _():
+            for k in range(2):
+                half_halo[k, side] = no_edge
+                field_halo[k, side] = no_edge
+                lower_half_rim[k, side] = no_row
+            lower_field_rim[side] = no_row
+            upper_field_rim[side] = no_row
+            still_rim[side] = jnp.zeros(still_rim.shape[1:], jnp.float32)
+            block_rim[side] = jnp.zeros(block_rim.shape[1:], jnp.float32)
+
+    for side, c in ((0, 0), (1, columns - 1)):
+        for d in range(depth):
+            still_edge[side, d] = right_ref[d, c : c + 1, :]
+            still_edge[side, depth + d] = cz_ref[d, c : c + 1, :]
+        still_edge[side, 2 * depth] = cx[c : c + 1, :]
 
     loads[0].wait()
     for d in range(depth):
@@ -113,6 +141,92 @@
             - upper_z[d] * pltpu.roll(v, cells - 1, 1)
         )
 
+    rim_lane = lax.broadcasted_iota(jnp.int32, (2, cells), 1)
+
+    def two(low, high):
+        pair_row = lax.broadcasted_iota(jnp.int32, (2, cells), 0)
+        return jnp.where(
+            pair_row == 0, jnp.broadcast_to(low, (2, cells)), jnp.broadcast_to(high, (2, cells))
+        )
+
+    def edges_of(v):
+        return two(v[:1], v[columns - 1 :])
+
+    def apply_rim(d, v):
+        parts = [None] * 4
+        for j in range(cells):
+            term = weights_rim[d, pl.ds(8 * j, 2), :] * jnp.broadcast_to(
+                v[:, j : j + 1], (2, cells)
+            )
+            parts[j % 4] = term if parts[j % 4] is None else parts[j % 4] + term
+        return relax * ((parts[0] + parts[1]) + (parts[2] + parts[3]))
+
+    def cx_rim():
+        return two(still_rim[0, 2 * depth], still_rim[1, 2 * depth])
+
+    def right_rim(d):
+        return two(still_rim[0, d], still_rim[1, d])
+
+    def column_rim(d, v):
+        cz = two(still_rim[0, depth + d], still_rim[1, depth + d])
+        above = pltpu.roll(cz, cells - 1, 1)
+        middle = 2.0 * cx_rim() + 2.0 * cy[d][:2] + cz + above
+        return (
+            middle * v
+            - jnp.where(rim_lane == 0, 0.0, cz) * pltpu.roll(v, 1, 1)
+            - jnp.where(rim_lane == cells - 1, 0.0, above) * pltpu.roll(v, cells - 1, 1)
+        )
+
+    def still_copies(side):
+        target = (w, p + (2 * side - 1))
+        return [
+            pltpu.make_async_remote_copy(
+                src_ref=source, dst_ref=aim, send_sem=send_still.at[2 * side + i],
+                recv_sem=recv_still.at[2 * side + i], device_id=target, device_id_type=MESH,
+            )
+            for i, (source, aim) in enumerate(
+                [
+                    (still_edge.at[side], still_rim.at[1 - side]),
+                    (block.at[:, 0 if side == 0 else columns - 1], block_rim.at[1 - side]),
+                ]
+            )
+        ]
+
+    def on_sides(action, arriving):
+        for side in range(2):
+            ok = (p > 0) if (side == 0) != arriving else (p < strips - 1)
+
+            @pl.when(ok)
+            def _():
+                action(side)
+
+    def start_still():
+        on_sides(lambda side: [c.start() for c in still_copies(side)], False)
+
+    def rim_ready():
+        on_sides(lambda side: [c.wait_recv() for c in still_copies(side)], True)
+        for side in range(2):
+            for d in range(depth):
+                weights_rim[d, pl.ds(side, cells, stride=8), :] = block_rim[side, d].T
+
+    def d_copy(source, target, side, slot, step):
+        return pltpu.make_async_remote_copy(
+            src_ref=source, dst_ref=target.at[1 - side],
+            send_sem=send_d.at[slot + side], recv_sem=recv_d.at[slot + side],
+            device_id=(w + step, p + (2 * side - 1)), device_id_type=MESH,
+        )
+
+    def up_half_rim(k):
+        return lambda side: d_copy(
+            half_edge.at[k, side, depth - 1], lower_half_rim.at[k], side, 2 * k, 1
+        )
+
+    def down_field_rim(side):
+        return d_copy(field_edge.at[0, side, 0], upper_field_rim, side, 4, -1)
+
+    def up_field_rim(side):
+        return d_copy(field_edge.at[0, side, depth - 1], lower_field_rim, side, 6, 1)
+
     def along_y(v, low, high):
         below = jnp.where(row == 0, low, pltpu.roll(v, 1, 0))
         above = jnp.where(row == columns - 1, high, pltpu.roll(v, columns - 1, 0))
@@ -131,11 +245,14 @@
             device_id=(w, p + (2 * side - 1)), device_id_type=MESH,
         )
 
-    def send_edges(planes, edges, halo, k, slot):
+    def store_edges(planes, edges, k):
         for d in range(depth):
             edges[k, 0, d] = planes[d][:1]
             edges[k, 1, d] = planes[d][columns - 1 :]
-
+            edges[k, 0, depth + d] = planes[d][1:2]
+            edges[k, 1, depth + d] = planes[d][columns - 2 : columns - 1]
+
+    def send_edges(edges, halo, k, slot):
         @pl.when(p > 0)
         def _():
             y_copy(edges, halo, k, 0, slot).start()
@@ -162,15 +279,19 @@
         def _():
             y_copy(edges, halo, k, 1, slot).wait_send()
 
-    def precondition(source, k, meanwhile):
+    def precondition(source, source_rim, k, meanwhile):
         slot = 3 * k
         edge_slot = 4 * k
+        ahead = RIM_FIRST or k == 1
         up_half = x_copy(half.at[k, depth - 1], from_lower_half.at[k], slot, 1)
         down_field = x_copy(field.at[k, 0], from_upper.at[k], slot + 1, -1)
         up_field = x_copy(field.at[k, depth - 1], from_lower.at[k], slot + 2, 1)
 
         @pl.when(w > 0)
         def _():
+            if k == 0:
+                pl.semaphore_wait(barrier, greeted)
+                start_still()
             up_half.wait_recv()
 
         lower = [from_lower_half[k]]
@@ -181,18 +302,55 @@
             half[k, d] = h[d]
 
         if k == 0:
-            pl.semaphore_wait(barrier, greeted)
+
+            @pl.when(w == 0)
+            def _():
+                pl.semaphore_wait(barrier, greeted)
 
         @pl.when(w < sections - 1)
         def _():
             up_half.start()
 
-        send_edges(h, half_edge, half_halo, k, edge_slot)
+        store_edges(h, half_edge, k)
+        if ahead:
+
+            @pl.when(w < sections - 1)
+            def _():
+                on_sides(lambda side: up_half_rim(k)(side).start(), False)
+
+        send_edges(half_edge, half_halo, k, edge_slot)
+        if k == 0:
+
+            @pl.when(w == 0)
+            def _():
+                start_still()
+
         meanwhile()
         partial = [source[d] - (column_part(d, h[d]) - cx * lower[d]) for d in range(depth)]
-        wait_edges(half_edge, half_halo, k, edge_slot)
+        if k == 0:
+            rim_ready()
+
+        def take_halo():
+            wait_edges(half_edge, half_halo, k, edge_slot)
+            for d in range(depth):
+                half_rim[d] = two(half_halo[k, 0, d], half_halo[k, 1, d])
+
+        if ahead:
+            pl.when(w == 0)(take_halo)
+
+            @pl.when(w > 0)
+            def _():
+                on_sides(lambda side: up_half_rim(k)(side).wait_recv(), True)
+                previous = two(lower_half_rim[k, 0], lower_half_rim[k, 1])
+                for d in range(depth):
+                    previous = apply_rim(d, source_rim(d) + cx_rim() * previous)
+                    half_rim[d] = previous
+
+        else:
+            take_halo()
+
         rest = [
-            partial[d] + cy[d] * along_y(h[d], half_halo[k, 0, d], half_halo[k, 1, d])
+            partial[d] + cy[d] * along_y(h[d], half_rim[d, 0:1], half_rim[d, 1:2])
             for d in range(depth)
         ]
 
@@ -218,12 +376,51 @@
         def _():
             up_field.start()
 
-        send_edges(z, field_edge, field_halo, k, edge_slot + 2)
+        store_edges(z, field_edge, k)
+        if k == 0:
+
+            @pl.when(w > 0)
+            def _():
+                on_sides(lambda side: down_field_rim(side).start(), False)
+
+            @pl.when(w < sections - 1)
+            def _():
+                on_sides(lambda side: up_field_rim(side).start(), False)
+
+        send_edges(field_edge, field_halo, k, edge_slot + 2)
+        if k == 0:
+
+            @pl.when(w < sections - 1)
+            def _():
+                on_sides(lambda side: down_field_rim(side).wait_recv(), True)
+
+            @pl.when(w == 0)
+            def _():
+                previous = two(upper_field_rim[0], upper_field_rim[1])
+                for d in reversed(range(depth)):
+                    v = half_rim[d]
+                    far = two(half_halo[0, 0, depth + d], half_halo[0, 1, depth + d])
+                    left = right_rim(d) - column_rim(d, v)
+                    left = left + cy[d][:2] * (far + edges_of(h[d]))
+                    if d > 0:
+                        left = left + cx_rim() * half_rim[d - 1]
+                    previous = v + apply_rim(d, left + cx_rim() * previous)
+                    field_rim[d] = previous
+
         return z, above, [column_part(d, z[d]) for d in range(depth)]
 
     def operate(k, z, above, partial):
         edge_slot = 4 * k
-        wait_edges(field_edge, field_halo, k, edge_slot + 2)
+
+        def take_halo():
+            wait_edges(field_edge, field_halo, k, edge_slot + 2)
+            for d in range(depth):
+                field_rim[d] = two(field_halo[k, 0, d], field_halo[k, 1, d])
+
+        if k == 0:
+            pl.when(w > 0)(take_halo)
+        else:
+            take_halo()
 
         @pl.when(w > 0)
         def _():
@@ -235,10 +432,29 @@
             image.append(
                 partial[d]
                 - cx * (below + above[d])
-                - cy[d] * along_y(z[d], field_halo[k, 0, d], field_halo[k, 1, d])
+                - cy[d] * along_y(z[d], field_rim[d, 0:1], field_rim[d, 1:2])
             )
             below = z[d]
         return image
+
+    def image_rim(z):
+        def at(d):
+            if d == 0:
+                on_sides(lambda side: up_field_rim(side).wait_recv(), True)
+            low = two(lower_field_rim[0], lower_field_rim[1]) if d == 0 else field_rim[d - 1]
+            high = (
+                two(upper_field_rim[0], upper_field_rim[1])
+                if d == depth - 1
+                else field_rim[d + 1]
+            )
+            far = two(field_halo[0, 0, depth + d], field_halo[0, 1, depth + d])
+            return (
+                column_rim(d, field_rim[d])
+                - cx_rim() * (low + high)
+                - cy[d][:2] * (far + edges_of(z[d]))
+            )
+
+        return at
 
     def finish(k):
         slot = 3 * k
@@ -252,6 +468,31 @@
         @pl.when(w > 0)
         def _():
             x_copy(field.at[k, 0], from_upper.at[k], slot + 1, -1).wait_send()
+
+        if RIM_FIRST or k == 1:
+
+            @pl.when(w > 0)
+            def _():
+                wait_edges(half_edge, half_halo, k, edge_slot)
+
+            @pl.when(w < sections - 1)
+            def _():
+                on_sides(lambda side: up_half_rim(k)(side).wait_send(), False)
+
+        if k == 0:
+            on_sides(lambda side: [c.wait_send() for c in still_copies(side)], False)
+
+            @pl.when(w == 0)
+            def _():
+                wait_edges(field_edge, field_halo, 0, 2)
+
+            @pl.when(w > 0)
+            def _():
+                on_sides(lambda side: down_field_rim(side).wait_send(), False)
+
+            @pl.when(w < sections - 1)
+            def _():
+                on_sides(lambda side: up_field_rim(side).wait_send(), False)
 
         wait_sent(half_edge, half_halo, k, edge_slot)
         wait_sent(field_edge, field_halo, k, edge_slot + 2)
@@ -265,7 +506,7 @@
     spot = lax.broadcasted_iota(jnp.int32, (1, cells), 1)
     rows = 1 + 2 * depth
     right = [right_ref[d] for d in range(depth)]
-    z, above, partial = precondition(right, 0, lambda: None)
+    z, above, partial = precondition(right, right_rim, 0, lambda: None)
     q = operate(0, z, above, partial)
 
     def early():
@@ -273,7 +514,7 @@
             spot == 0, inner(z, right), jnp.where(spot == 1, inner(z, q), 0.0)
         )
 
-    y, above, partial = precondition(q, 1, early)
+    y, above, partial = precondition(q, image_rim(z), 1, early)
     faced = []
     for d in range(depth):
         next_column = jnp.where(row == columns - 1, 0.0, pltpu.roll(y[d], columns - 1, 0))
@@ -381,13 +622,22 @@
                 pltpu.VMEM((depth, cells * columns, cells), jnp.float32),
                 pltpu.VMEM((2, depth) + plane, jnp.float32),
                 pltpu.VMEM((2, depth) + plane, jnp.float32),
-                pltpu.VMEM((2, 2, depth, 1, cells), jnp.float32),
-                pltpu.VMEM((2, 2, depth, 1, cells), jnp.float32),
+                pltpu.VMEM((2, 2, 2 * depth, 1, cells), jnp.float32),
+                pltpu.VMEM((2, 2, 2 * depth, 1, cells), jnp.float32),
                 pltpu.VMEM((2,) + plane, jnp.float32),
                 pltpu.VMEM((2,) + plane, jnp.float32),
                 pltpu.VMEM((2,) + plane, jnp.float32),
-                pltpu.VMEM((2, 2, depth, 1, cells), jnp.float32),
-                pltpu.VMEM((2, 2, depth, 1, cells), jnp.float32),
+                pltpu.VMEM((2, 2, 2 * depth, 1, cells), jnp.float32),
+                pltpu.VMEM((2, 2, 2 * depth, 1, cells), jnp.float32),
+                pltpu.VMEM((2, 2 * depth + 1, 1, cells), jnp.float32),
+                pltpu.VMEM((2, 2 * depth + 1, 1, cells), jnp.float32),
+                pltpu.VMEM((2, depth, cells, cells), jnp.float32),
+                pltpu.VMEM((depth, 8 * cells, cells), jnp.float32),
+                pltpu.VMEM((depth, 2, cells), jnp.float32),
+                pltpu.VMEM((depth, 2, cells), jnp.float32),
+                pltpu.VMEM((2, 2, 1, cells), jnp.float32),
+                pltpu.VMEM((2, 1, cells), jnp.float32),
+                pltpu.VMEM((2, 1, cells), jnp.float32),
                 pltpu.VMEM((2, rows, 1, cells), jnp.float32),
                 pltpu.VMEM((slots, rows, 1, cells), jnp.float32),
                 pltpu.SemaphoreType.DMA((5,)),
@@ -395,6 +645,10 @@
                 pltpu.SemaphoreType.DMA((6,)),
                 pltpu.SemaphoreType.DMA((8,)),
                 pltpu.SemaphoreType.DMA((8,)),
+                pltpu.SemaphoreType.DMA((8,)),
+                pltpu.SemaphoreType.DMA((8,)),
+                pltpu.SemaphoreType.DMA((4,)),
+                pltpu.SemaphoreType.DMA((4,)),
                 pltpu.SemaphoreType.DMA((slots,)),
                 pltpu.SemaphoreType.DMA((slots,)),
             ],

time: 31.3 us -> 29.2 us (0.933)
  Pallas kernels: 29.3 us -> 27.2 us
    pallas_call x1, Pallas kernels: 29.3 us -> 27.2 us  [on_device(): pl.pallas_call(functools.partial(kernel, sections, strips), out_shape=(ou...]
where the time goes in v3:
time: 29.2 us; the launch traced here: 29.1 us
  Pallas kernels  27.2 us (93%)
  local copies, waits for them, and re-layouts  1.19 us (4%)
  between operations  0.64 us (2%)
    pallas_call x1, Pallas kernels, on_device(): pl.pallas_call(functools.partial(kernel, sections, strips), out_shape=(ou...  27.2 us
    unnamed x2, local copies, waits for them, and re-layouts  1.19 us

profile of v3, /device:TPU:0, one launch (start us, length us, event | category | flops | bytes accessed | tf_op | source)
XLA Modules:
  0.0 29.1 jit_solution(273258041570943541)
XLA Ops:
  0.6 27.2 %shard_map.68 = (f32[1,8,128]{2,1,0:T(8,128)S(1)}, f32[1,8,128]{2,1,0:T(8,128)S(1)}) custom-call(f32[1,8,128]{2,1,0:T(8,128)} %right_any.1, f32[8,128]{1,0:T(8,128)} %cx_any.1, f32[1,128]{1,0:T(1,128)} %cy_any.1, f32[1,8,128]{2,1,0:T(8,128)} %cz_any.1, f32[1,8,128,128]{3,2,1,0:T(8,128)} %inverse_any.1), custom_call_target="tpu_custom_call" | custom-call | tf_op jit(solution)/shard_map/pallas_call | solution.py:611
  27.9 0.6 %copy.9 = f32[1,8,128]{2,1,0:T(8,128)} copy(f32[1,8,128]{2,1,0:T(8,128)S(1)} %get-tuple-element.2) | data formatting | bytes 8192
  28.5 0.6 %copy.10 = f32[1,8,128]{2,1,0:T(8,128)} copy(f32[1,8,128]{2,1,0:T(8,128)S(1)} %get-tuple-element.3) | data formatting | bytes 8192

commit v4 on v3

--- a/solution.py
+++ b/solution.py
@@ -10,7 +10,7 @@
 relax = 1.5
 MESH = pl.DeviceIdType.MESH
 DIRECT = 64
-RIM_FIRST = False
+RIM_FIRST = True
 
 
 def kernel(

time: 29.2 us -> 27.4 us (0.938)
  Pallas kernels: 27.2 us -> 25.4 us
    pallas_call x1, Pallas kernels: 27.2 us -> 25.4 us  [on_device(): pl.pallas_call(functools.partial(kernel, sections, strips), out_shape=(ou...]
where the time goes in v4:
time: 27.4 us; the launch traced here: 27.2 us
  Pallas kernels  25.4 us (93%)
  local copies, waits for them, and re-layouts  1.19 us (4%)
  between operations  0.64 us (2%)
    pallas_call x1, Pallas kernels, on_device(): pl.pallas_call(functools.partial(kernel, sections, strips), out_shape=(ou...  25.4 us
    unnamed x2, local copies, waits for them, and re-layouts  1.19 us

profile of v4, /device:TPU:0, one launch (start us, length us, event | category | flops | bytes accessed | tf_op | source)
XLA Modules:
  0.0 27.2 jit_solution(8646882110449872192)
XLA Ops:
  0.6 25.4 %shard_map.68 = (f32[1,8,128]{2,1,0:T(8,128)S(1)}, f32[1,8,128]{2,1,0:T(8,128)S(1)}) custom-call(f32[1,8,128]{2,1,0:T(8,128)} %right_any.1, f32[8,128]{1,0:T(8,128)} %cx_any.1, f32[1,128]{1,0:T(1,128)} %cy_any.1, f32[1,8,128]{2,1,0:T(8,128)} %cz_any.1, f32[1,8,128,128]{3,2,1,0:T(8,128)} %inverse_any.1), custom_call_target="tpu_custom_call" | custom-call | tf_op jit(solution)/shard_map/pallas_call | solution.py:611
  26.1 0.6 %copy.9 = f32[1,8,128]{2,1,0:T(8,128)} copy(f32[1,8,128]{2,1,0:T(8,128)S(1)} %get-tuple-element.2) | data formatting | bytes 8192
  26.7 0.6 %copy.10 = f32[1,8,128]{2,1,0:T(8,128)} copy(f32[1,8,128]{2,1,0:T(8,128)S(1)} %get-tuple-element.3) | data formatting | bytes 8192
